TPU v7x, 8 devices: a whole 2x2x1 slice. The times are simulated.
8 devices in a mesh: tp: 4 (over z, y, x), dp: 2 (over core).
Axes of the slice: x: 2, y: 2, z: 1, core: 2. Of those that a mesh axis runs over, the one named last changes fastest.
Arguments:
- hidden: bfloat16 [2, 1024, 1024], P('dp')
- gain: float32 [1024], replicated
- embedding: bfloat16 [250112, 1024], P('tp')
- targets: int32 [2, 1024], P('dp')
- weights: float32 [2, 1024], P('dp')
Outputs:
- output 1: float32 [], replicated
- output 2: bfloat16 [2, 1024, 1024], P('dp')
- output 3: float32 [250112, 1024], P('tp')
- output 4: float32 [1024], replicated
All inputs are finite; a program needn't handle non-finite values.
Results may differ from a plain program's by a relative error of at most 0.001.
Values sent between devices are 32-bit elements.
A program may use at most 1.5 GiB of HBM per device.

v0:
```python
import jax
import jax.numpy as jnp
from jax import lax
from jax.sharding import PartitionSpec as P

LN_EPS = 1e-6
Z_COEF = 1e-4


def solution(mesh):
    def local_step(hidden, gain, emb_rows, targets, weights):
        vocab_rows = emb_rows.shape[0]
        hid_f32 = hidden.astype(jnp.float32)
        centered = hid_f32 - hid_f32.mean(-1, keepdims=True)
        inv_std = lax.rsqrt((centered * centered).mean(-1, keepdims=True) + LN_EPS)
        x_hat = centered * inv_std
        normed = (x_hat * gain).astype(jnp.bfloat16)
        logits = jnp.einsum('bsd,vd->bsv', normed, emb_rows, preferred_element_type=jnp.float32)
        peak = lax.pmax(logits.max(-1), 'tp')
        exp_sum = lax.psum(jnp.exp(logits - peak[..., None]).sum(-1), 'tp')
        log_z = peak + jnp.log(exp_sum)
        local_ids = targets - lax.axis_index('tp') * vocab_rows
        is_target = lax.broadcasted_iota(jnp.int32, (1, 1, vocab_rows), 2) == local_ids[..., None]
        tgt_logit = lax.psum(jnp.where(is_target, logits, 0.0).sum(-1), 'tp')
        w_total = lax.psum(weights.sum(), 'dp')
        tok_scale = weights / w_total
        loss = lax.psum((tok_scale * (log_z - tgt_logit + Z_COEF * log_z * log_z)).sum(), 'dp')
        soft_probs = jnp.exp(logits - log_z[..., None])
        grad_logits = ((soft_probs * (1.0 + 2.0 * Z_COEF * log_z)[..., None] - is_target.astype(jnp.float32)) * tok_scale[..., None]).astype(jnp.bfloat16)
        d_normed = lax.psum(jnp.einsum('bsv,vd->bsd', grad_logits, emb_rows, preferred_element_type=jnp.float32), 'tp')
        d_emb = lax.psum(jnp.einsum('bsv,bsd->vd', grad_logits, normed, preferred_element_type=jnp.float32), 'dp')
        d_gain = lax.psum((d_normed * x_hat).sum((0, 1)), 'dp')
        value_a6 = d_normed * gain
        d_hidden = inv_std * (value_a6 - value_a6.mean(-1, keepdims=True) - x_hat * (value_a6 * x_hat).mean(-1, keepdims=True))
        return loss, d_hidden.astype(jnp.bfloat16), d_emb, d_gain

    return jax.shard_map(local_step, mesh=mesh,
                         in_specs=(P('dp', None, None), P(None), P('tp', None), P('dp', None), P('dp', None)),
                         out_specs=(P(), P('dp', None, None), P('tp', None), P(None)),
                         check_vma=False)
```

profile of v0, /device:TPU:0, one launch (start us, length us, event | category | flops | bytes accessed | tf_op | source)
XLA Modules:
  0.0 1380.0 jit_solution(15828919014384059222)
XLA Ops:
  7.2 0.0 copy-start
  7.2 0.0 copy-start.6
  7.2 0.0 all-reduce.5.cloned.1.call-start
  7.2 2.1 convert_reduce_fusion
  9.3 0.0 copy-start.2
  9.3 2.3 fusion.12
  11.6 0.0 copy-done.2
  11.6 0.0 copy-start.4
  11.6 0.6 copy-done.4
  12.2 0.0 copy-done
  12.2 0.0 copy-done.6
  12.2 2.0 fusion.20.clone.4
  14.2 0.0 copy-start.9
  14.2 149.9 %fusion.21 = (f32[1024]{0:T(1024)S(1)}, f32[1024,62528]{0,1:T(8,128)}) fusion(bf16[62528,1024]{1,0:T(8,128)(2,1)} %param.7, bf16[1024,1024]{1,0:T(8,128)(2,1)} %fusion.20.clone.4), kind=kOutput, calls=%fused_computation.36 | convolution fusion | flops 131194748928 | bytes 386273280 | tf_op jit(solution)/shard_map/bsd,vd->bsv/dot_general | solution.py:18
  164.1 11.7 pmax.7
  175.8 0.0 copy-done.9
  175.9 0.0 copy-start.8
  175.9 76.1 %select_reduce_fusion = (f32[1024]{0:T(1024)S(1)}, f32[1024]{0:T(1024)S(1)}) fusion(f32[1024,62528]{0,1:T(8,128)} %get-tuple-element.18, s32[1024]{0:T(1024)S(1)} %bitcast.29, f32[1024]{0:T(1024)S(1)} %bitcast.28), kind=kLoop, calls=%fused_computation.1 | loop fusion | flops 320141312 | bytes 256131072 | tf_op jit(solution)/shard_map/reduce_sum | solution.py:24
  251.9 8.2 all-reduce
  260.2 0.0 copy-done.8
  260.2 0.6 reduce_sum.85
  260.8 3.1 psum.49
  263.9 1.3 fusion.16
  265.2 176.4 %convolution_bitcast_fusion = f32[1,1024,1024]{2,1,0:T(8,128)} fusion(bf16[62528,1024]{1,0:T(8,128)(2,1)} %param.7, f32[1024,62528]{0,1:T(8,128)} %get-tuple-element.18, f32[1024]{0:T(1024)S(1)} %bitcast.36, f32[1024]{0:T(1024)S(1)} %bitcast.39, f32[1024]{0:T(1024)S(1)} %bitcast.34, s32[1024]{0:T(1024)S(1)} %bitcast.30), kind=kOutput, calls=%fused_computation.20 | convolution fusion | flops 131578920960 | bytes 388382720 | tf_op jit(solution)/shard_map/bsv,vd->bsd/dot_general | solution.py:30
  441.5 0.0 copy-start.1
  441.5 0.0 copy-start.3
  441.5 0.0 copy-start.5
  441.5 0.0 copy-start.7
  441.5 0.0 all-reduce.5.cloned.1.call-update
  441.6 0.3 all-reduce.7.cloned.1.call-start
  441.8 1.3 copy-done.1
  443.1 0.0 copy-done.3
  443.1 0.0 copy-done.5
  443.1 0.0 copy-done.7
  443.1 189.0 %fusion.17 = f32[62528,1024]{1,0:T(8,128)} fusion(bf16[1,1024,1024]{2,1,0:T(8,128)(2,1)S(1)} %copy-done.1, f32[1024]{0:T(1024)S(1)} %copy-done.7, f32[1024]{0:T(1024)S(1)} %copy-done.5, f32[1024]{0:T(1024)S(1)} %copy-done.3, f32[1024,62528]{0,1:T(8,128)} %get-tuple-element.18, f32[1024]{0:T(1024)S(1)} %bitcast.37, f32[1024]{0:T(1024)S(1)} %bitcast.40, ...), kind=kOutput, calls=%fused_computation.34 | convolution fusion | flops 131584163840 | bytes 514355200 | tf_op jit(solution)/shard_map/bsv,bsd->vd/dot_general | solution.py:31
  632.1 0.0 all-reduce.7.cloned.1.call-update
  632.1 0.0 all-reduce.5.cloned.1.call-done
  632.2 3.6 fusion.11
  635.7 3.2 all-reduce.1
  639.0 3.9 fusion.10
  642.9 564.4 %all-reduce.7.cloned.1.call-done = f32[62528,1024]{1,0:T(8,128)} async-done(((f32[62528,1024]{1,0:T(8,128)}), f32[62528,1024]{1,0:T(8,128)}) %all-reduce.7.cloned.1.call-update) | async-done | bytes 256114704 | tf_op jit(solution)/shard_map/psum | solution.py:31
  1207.3 165.8 %copy.11 = f32[62528,1024]{1,0:T(8,128)} copy(f32[62528,1024]{1,0:T(8,128)} %all-reduce.7.cloned.1.call-done) | data formatting | bytes 512229376
  (5 shorter events, 0.0 us)
Async XLA Ops:
  7.2 5.1 copy-start
  7.2 5.1 copy-start.6
  7.2 625.0 %all-reduce.5.cloned.1.call-start = ((), (), s32[]{:S(2)}) async-start(), calls=%async_computation | async-start | bytes 8388608 | tf_op jit(solution)/shard_map/psum | solution.py:30
  9.3 2.3 copy-start.2
  11.6 0.6 copy-start.4
  14.2 161.6 %copy-start.9 = (s32[1,1024]{1,0:T(1,128)S(1)}, s32[1,1024]{1,0:T(1,128)}, u32[]{:S(2)}) copy-start(s32[1,1024]{1,0:T(1,128)} %param.8) | copy-start | bytes 12292
  175.9 84.3 %copy-start.8 = (f32[1,1024]{1,0:T(1,128)S(1)}, f32[1,1024]{1,0:T(1,128)}, u32[]{:S(2)}) copy-start(f32[1,1024]{1,0:T(1,128)} %param.9) | copy-start | bytes 12292
  441.5 1.6 copy-start.1
  441.5 1.6 copy-start.3
  441.5 1.6 copy-start.5
  441.5 1.6 copy-start.7
  441.6 765.8 %all-reduce.7.cloned.1.call-start = ((), (), s32[]{:S(2)}) async-start(), calls=%async_computation.1 | async-start | bytes 512229376 | tf_op jit(solution)/shard_map/psum | solution.py:31
Sparse Core Ops, SparseCore 0:
  441.7 91.9 all-reduce.4
  632.2 575.0 all-reduce.6
where the time goes:
time: 1380 us
  waiting for transfers between devices  564 us (41%)
  matrix products  515 us (37%)
  local copies, waits for them, and re-layouts  168 us (12%)
  other arithmetic  91.8 us (7%)
  blocking collectives  26.3 us (2%)
  between operations  14.2 us (1%)
    psum x1, waiting for transfers between devices, local_step(): lax.psum(jnp.einsum('bsv,bsd->vd', grad_logits, normed, preferred_element...  564 us
    dot_general x1, matrix products, local_step(): jnp.einsum('bsv,bsd->vd', grad_logits, normed, preferred_element_type=jnp...  189 us
    dot_general x1, matrix products, local_step(): jnp.einsum('bsv,vd->bsd', grad_logits, emb_rows, preferred_element_type=j...  176 us
    unnamed x21, local copies, waits for them, and re-layouts  168 us
    dot_general x1, matrix products, local_step(): jnp.einsum('bsd,vd->bsv', normed, emb_rows, preferred_element_type=jnp.fl...  150 us
    reduce_sum x1, other arithmetic, local_step(): tgt_logit = lax.psum(jnp.where(is_target, logits, 0.0).sum(-1), 'tp')  76.1 us
  transfers between devices with their start and end apart: 2, of which 1 were waited for; matrix products, arithmetic and copies ran while one was open for 14% of the time, Pallas kernels for 0%

commit v1 on v0

v1 whole, which is shorter than its diff:
```python
import functools

import jax
import jax.numpy as jnp
from jax import lax
from jax.experimental import pallas as pl
from jax.experimental.pallas import tpu as pltpu
from jax.sharding import PartitionSpec as P

LN_EPS = 1e-6
Z_COEF = 1e-4
TILE = 1024
SUB = 256
BLOCK = 256
LANES = 128
STAT_SUB = 128
SPAN = 512
NEG = -3.0e38
SENT = {5: (15, 15), 6: (17, 8), 7: (18, 9), 8: (19, 8)}
F32 = jnp.float32
BF16 = jnp.bfloat16


def _dot(a, b):
    return jnp.dot(a, b, preferred_element_type=F32)


def _tree(op, parts):
    while len(parts) > 1:
        parts = [op(a, b) for a, b in zip(parts[::2], parts[1::2])] + ([parts[-1]] if len(parts) % 2 else [])
    return parts[0]


def _stats(r, sub, cols, first_row, log_ref, tgt_ref, m_ref, s_ref, tl_ref):
    ids = tgt_ref[:, cols] - (first_row + r) - lax.broadcasted_iota(jnp.int32, (8, LANES), 0)
    tl_ref[:, cols] += _tree(jnp.add, [jnp.where(ids == k, log_ref[r + k:r + k + 8, cols], 0.0) for k in range(0, sub, 8)])
    old = m_ref[:, cols]
    new = jnp.maximum(old, _tree(jnp.maximum, [log_ref[r + k:r + k + 8, cols] for k in range(0, sub, 8)]))
    total = _tree(jnp.add, [jnp.exp(log_ref[r + k:r + k + 8, cols] - new) for k in range(0, sub, 8)])
    s_ref[:, cols] = s_ref[:, cols] * jnp.exp(old - new) + total
    m_ref[:, cols] = new


def _columns(tokens):
    return [slice(c, c + LANES) for c in range(0, tokens, LANES)]


def _logits_body(rows, tokens, first_row, emb_ref, yft_ref, tgt_ref, log_ref, m_ref, s_ref, tl_ref):
    sub = min(rows, STAT_SUB)
    for r in range(0, rows + sub, sub):
        if r < rows:
            log_ref[r:r + sub, :] = _dot(emb_ref[r:r + sub, :], yft_ref[...])
        if r > 0:
            for cols in _columns(tokens):
                _stats(r - sub, sub, cols, first_row, log_ref, tgt_ref, m_ref, s_ref, tl_ref)


def _logits_kernel(tokens, last, rest, base_ref, emb_ref, yft_ref, tgt_ref, log_ref, m_ref, s_ref, tl_ref):
    tile = base_ref[0] + pl.program_id(0)

    @pl.when(pl.program_id(0) == 0)
    def _():
        m_ref[...] = jnp.full_like(m_ref, NEG)
        s_ref[...] = jnp.zeros_like(s_ref)
        tl_ref[...] = jnp.zeros_like(tl_ref)

    body = functools.partial(_logits_body, tokens=tokens, first_row=tile * TILE, emb_ref=emb_ref, yft_ref=yft_ref, tgt_ref=tgt_ref,
                             log_ref=log_ref, m_ref=m_ref, s_ref=s_ref, tl_ref=tl_ref)
    pl.when(tile != last)(lambda: body(TILE))
    pl.when(tile == last)(lambda: body(rest))


def _grad_columns(r, sub, cols, first_row, log_ref, vec_ref, tgt_ref, g_ref):
    log_z, scale, weight = vec_ref[0:1, cols], vec_ref[1:2, cols], vec_ref[2:3, cols]
    ids = tgt_ref[0:1, cols] - (first_row + r)
    step = min(sub, 64)
    row = lax.broadcasted_iota(jnp.int32, (step, LANES), 0)
    for k in range(0, sub, step):
        prob = jnp.exp(log_ref[r + k:r + k + step, cols] - log_z)
        grad = prob * scale - jnp.where(row == ids - k, weight, 0.0)
        g_ref[r + k:r + k + step, cols] = grad.astype(BF16)


def _emb_grad(r, sub, width, jobs, yf_ref, g_ref, de_refs):
    spans = range(0, width, SPAN)
    for n, c in enumerate(spans):
        part = _dot(g_ref[r:r + sub, :], yf_ref[:, c:c + SPAN])
        for de_ref in de_refs:
            de_ref[r:r + sub, c:c + SPAN] = part
        for job in jobs[n::len(spans)]:
            job()


def _column_jobs(r, rows, sub, tokens, *args):
    return [functools.partial(_grad_columns, r, sub, cols, *args) for cols in _columns(tokens)] if r < rows else []


def _own_body(rows, tokens, first_row, log_ref, emb_ref, yf_ref, vec_ref, tgt_ref, de_refs, dyf_ref, g_ref):
    sub = min(rows, SUB)
    width = yf_ref.shape[1]
    jobs = lambda r: _column_jobs(r, rows, sub, tokens, first_row, log_ref, vec_ref, tgt_ref, g_ref)
    for job in jobs(0):
        job()
    for r in range(0, rows, sub):
        _emb_grad(r, sub, width, jobs(r + sub), yf_ref, g_ref, de_refs)
    for c in range(0, width, SUB):
        dyf_ref[c:c + SUB, :] += lax.dot_general(emb_ref[0:rows, c:c + SUB], g_ref[0:rows, :], (((0,), (0,)), ((), ())),
                                                 preferred_element_type=F32)


def _own_kernel(tokens, last, rest, first, base_ref, log_ref, emb_ref, yf_ref, vec_ref, tgt_ref, *refs):
    if first:
        de_ref, dyf_ref, copy_ref, g_ref = refs
        de_refs = [de_ref, copy_ref]
    else:
        _, before_ref, de_ref, dyf_ref, g_ref = refs
        de_refs = [de_ref]
    tile = base_ref[0] + pl.program_id(0)

    @pl.when(pl.program_id(0) == 0)
    def _():
        dyf_ref[...] = jnp.zeros_like(dyf_ref) if first else before_ref[...]

    body = functools.partial(_own_body, tokens=tokens, first_row=tile * TILE, log_ref=log_ref, emb_ref=emb_ref, yf_ref=yf_ref,
                             vec_ref=vec_ref, tgt_ref=tgt_ref, de_refs=de_refs, dyf_ref=dyf_ref, g_ref=g_ref)
    if first:
        body(TILE)
    else:
        pl.when(tile != last)(lambda: body(TILE))
        pl.when(tile == last)(lambda: body(rest))


def _peer_body(rows, tokens, first_row, emb_ref, yft_ref, yf_ref, vec_ref, tgt_ref, de_ref, g_ref, log_ref):
    sub = min(rows, SUB)
    jobs = lambda r: _column_jobs(r, rows, sub, tokens, first_row, log_ref, vec_ref, tgt_ref, g_ref)

    def logits(r):
        if r < rows:
            log_ref[r:r + sub, :] = _dot(emb_ref[r:r + sub, :], yft_ref[...])

    logits(0)
    logits(sub)
    for job in jobs(0):
        job()
    for r in range(0, rows, sub):
        logits(r + 2 * sub)
        _emb_grad(r, sub, yf_ref.shape[1], jobs(r + sub), yf_ref, g_ref, [de_ref])


def _peer_kernel(tokens, last, rest, sent, pieces, base_ref, emb_ref, got_ref, yft_ref, yf_ref, vec_ref, tgt_ref, _, out_ref,
                 g_ref, log_ref, de_ref, sems):
    i = pl.program_id(0)
    slot = i % 2
    tile = base_ref[0] + sent + i
    body = functools.partial(_peer_body, tokens=tokens, first_row=tile * TILE, emb_ref=emb_ref, yft_ref=yft_ref, yf_ref=yf_ref,
                             vec_ref=vec_ref, tgt_ref=tgt_ref, de_ref=de_ref.at[slot], g_ref=g_ref, log_ref=log_ref)

    def store(which, rows, start=0):
        return pltpu.make_async_copy(de_ref.at[which, pl.ds(0, rows)], out_ref.at[pl.ds(start, rows)], sems.at[which])

    size = got_ref.shape[0]
    piece = pltpu.make_async_copy(got_ref, out_ref.at[pl.ds(base_ref[0] * TILE + jnp.minimum(i, pieces - 1) * size, size)], sems.at[2])
    pl.when(i < pieces)(lambda: piece.start())
    pl.when(i >= 2)(lambda: store(slot, TILE).wait())

    @pl.when(tile != last)
    def _():
        body(TILE)
        store(slot, TILE, tile * TILE).start()

    @pl.when(tile == last)
    def _():
        body(rest)
        store(slot, rest, tile * TILE).start()
        store(slot, rest).wait()

    pl.when(i < pieces)(lambda: piece.wait())

    @pl.when(i == pl.num_programs(0) - 1)
    def _():
        store(1 - slot, TILE).wait()
        pl.when(tile != last)(lambda: store(slot, TILE).wait())


def solution(mesh):
    def local_step(hidden, gain, emb_rows, targets, weights):
        vocab_rows, width = emb_rows.shape
        seq = hidden.shape[1]
        last, rest = vocab_rows // TILE, vocab_rows % TILE
        half = pl.cdiv(pl.cdiv(vocab_rows, TILE), 2)
        me = lax.axis_index('dp')
        swap = functools.partial(lax.ppermute, axis_name='dp', perm=[(0, 1), (1, 0)])

        hid_f32 = hidden[0].astype(F32)
        centered = hid_f32 - hid_f32.mean(-1, keepdims=True)
        inv_std = lax.rsqrt((centered * centered).mean(-1, keepdims=True) + LN_EPS)
        x_hat = centered * inv_std

        def both(mine, other):
            return jnp.where(me == 0, mine, other), jnp.where(me == 0, other, mine)

        x0, x1 = both(x_hat, swap(x_hat))
        t0, t1 = both(targets[0], swap(targets[0]))
        w0, w1 = both(weights[0], swap(weights[0]))
        n0 = w0.sum().astype(jnp.int32)
        n1 = w1.sum().astype(jnp.int32)
        blocks0, blocks1 = (n0 + BLOCK - 1) // BLOCK, (n1 + BLOCK - 1) // BLOCK
        start1 = blocks0 * BLOCK
        w_total = w0.sum() + w1.sum()

        def pack(a, b):
            zero = jnp.zeros_like(a)
            moved = lax.dynamic_slice(jnp.concatenate([zero, b, zero], 0), (seq - start1,) + (0,) * (a.ndim - 1), (2 * seq,) + a.shape[1:])
            first = lax.broadcasted_iota(jnp.int32, (2 * seq,) + (1,) * (a.ndim - 1), 0) < start1
            return jnp.where(first, jnp.concatenate([a, zero], 0), moved)

        yf = pack((x0 * gain).astype(BF16), (x1 * gain).astype(BF16))
        tok_scale = pack(w0, w1) / w_total
        local_ids = pack(t0, t1) - lax.axis_index('tp') * vocab_rows
        base_own = jnp.full((1,), half, jnp.int32) * me
        base_peer = jnp.full((1,), half, jnp.int32) * (1 - me)

        def branch(tokens):
            def run(yf, tok_scale, local_ids, emb_rows, base_own, base_peer):
                yf, tok_scale, local_ids = yf[:tokens], tok_scale[:tokens], local_ids[:tokens]
                yft = yf.T
                any_spec = pl.BlockSpec(memory_space=pl.ANY)
                one = pl.Buffered(1)
                row = lambda i, b: (b[0] + i, 0)
                near = lambda i, b: (i, 0)
                fixed = lambda i, b: (0, 0)
                emb_spec = pl.BlockSpec((TILE, width), row)
                yft_spec = pl.BlockSpec((width, tokens), fixed, pipeline_mode=one)
                yf_spec = pl.BlockSpec((tokens, width), fixed, pipeline_mode=one)
                log_spec = pl.BlockSpec((TILE, tokens), near)
                vec_spec = pl.BlockSpec((8, tokens), fixed)
                vec_shape = jax.ShapeDtypeStruct((8, tokens), F32)
                de_shape = jax.ShapeDtypeStruct((vocab_rows, width), F32)
                g_scratch = pltpu.VMEM((TILE, tokens), BF16)
                params = pltpu.CompilerParams(dimension_semantics=('arbitrary',), vmem_limit_bytes=62 * 2**20)

                sent, pieces = SENT[tokens // BLOCK]
                size = sent * TILE // pieces

                def call(kernel, name, dots, scalars, steps, ins, outs, shapes, scratch=(), args=(), **kw):
                    return pl.pallas_call(
                        functools.partial(kernel, tokens, last, rest, *args),
                        grid_spec=pltpu.PrefetchScalarGridSpec(num_scalar_prefetch=1, grid=(steps,), in_specs=ins, out_specs=outs,
                                                               scratch_shapes=scratch),
                        out_shape=shapes, compiler_params=params, name=name,
                        cost_estimate=pl.CostEstimate(flops=2 * dots * steps * TILE * tokens * width, transcendentals=0,
                                                      bytes_accessed=steps * TILE * (tokens + 2 * width) * 4), **kw)

                tgt = jnp.broadcast_to(local_ids[None], (8, tokens))
                logits, m, s, tl = call(_logits_kernel, 'logits', 1, base_own, half, [emb_spec, yft_spec, vec_spec],
                                        [log_spec, vec_spec, vec_spec, vec_spec],
                                        [jax.ShapeDtypeStruct((half * TILE, tokens), F32), vec_shape, vec_shape, vec_shape])(
                                            base_own, emb_rows, yft, tgt)
                m_dev = m.max(0)
                s_dev = (s * jnp.exp(m - m_dev[None])).sum(0)
                stats = lax.all_gather(jnp.stack([m_dev, s_dev, tl.sum(0)]), ('tp', 'dp'))
                peak = stats[:, 0].max(0)
                log_z = peak + jnp.log((stats[:, 1] * jnp.exp(stats[:, 0] - peak[None])).sum(0))
                loss = (tok_scale * (log_z - stats[:, 2].sum(0) + Z_COEF * log_z * log_z)).sum()
                vec = jnp.stack([log_z, (1.0 + 2.0 * Z_COEF * log_z) * tok_scale, tok_scale] + [tok_scale] * 5)

                dyf_spec = pl.BlockSpec((width, tokens), fixed, pipeline_mode=one)
                dyf_shape = jax.ShapeDtypeStruct((width, tokens), F32)
                later_spec = pl.BlockSpec((TILE, tokens), lambda i, b: (sent + i, 0))
                own_ins = [emb_spec, yf_spec, vec_spec, vec_spec]
                d_emb, dyf_a, send = call(_own_kernel, 'grads_first', 2, base_own, sent, [log_spec] + own_ins,
                                          [emb_spec, dyf_spec, pl.BlockSpec((TILE, width), near)],
                                          [de_shape, dyf_shape, jax.ShapeDtypeStruct((sent * TILE, width), F32)],
                                          [g_scratch], (True,))(base_own, logits, emb_rows, yf, vec, tgt)
                got = swap(send)
                d_emb, dyf_b = call(_own_kernel, 'grads_own', 2, base_own, half - sent, [later_spec] + own_ins + [any_spec, dyf_spec],
                                    [emb_spec, dyf_spec], [de_shape, dyf_shape], [g_scratch], (False,),
                                    input_output_aliases={6: 0})(base_own + sent, logits, emb_rows, yf, vec, tgt, d_emb, dyf_a)
                d_part = dyf_b.T
                d0 = d_part[:seq]
                d1 = lax.dynamic_slice(jnp.pad(d_part, ((0, 2 * seq - tokens), (0, 0))), (start1, 0), (seq, width))
                d_sum = lax.psum(jnp.where(me == 0, d0, d1) + swap(jnp.where(me == 0, d1, d0)), 'tp')
                d_emb = call(_peer_kernel, 'grads_peer', 2, base_peer, half - sent,
                             [pl.BlockSpec((TILE, width), lambda i, b: (b[0] + sent + i, 0)),
                              pl.BlockSpec((size, width), lambda i, b: (jnp.minimum(i, pieces - 1), 0)),
                              yft_spec, yf_spec, vec_spec, vec_spec, any_spec],
                             any_spec, de_shape,
                             [g_scratch, pltpu.VMEM((TILE, tokens), F32), pltpu.VMEM((2, TILE, width), F32), pltpu.SemaphoreType.DMA((3,))],
                             (sent, pieces), input_output_aliases={7: 0})(base_peer, emb_rows, got, yft, yf, vec, tgt, d_emb)
                d_emb, d_sum = lax.optimization_barrier((d_emb, d_sum))
                return d_emb, d_sum, loss
            return run

        sizes = range(5 * BLOCK, 2 * seq + 1, BLOCK)
        which = jnp.clip(blocks0 + blocks1 - 5, 0, len(sizes) - 1)
        d_emb, d_normed, loss = lax.switch(which, [branch(n) for n in sizes], yf, tok_scale, local_ids, emb_rows, base_own, base_peer)

        d_normed = jnp.where(weights[0][:, None] > 0, d_normed, 0.0)
        d_gain = (d_normed * x_hat).sum(0)
        d_gain = d_gain + swap(d_gain)
        d_rows = d_normed * gain
        d_hidden = inv_std * (d_rows - d_rows.mean(-1, keepdims=True) - x_hat * (d_rows * x_hat).mean(-1, keepdims=True))
        return loss, d_hidden.astype(BF16)[None], d_emb, d_gain

    return jax.shard_map(local_step, mesh=mesh,
                         in_specs=(P('dp', None, None), P(None), P('tp', None), P('dp', None), P('dp', None)),
                         out_specs=(P(), P('dp', None, None), P('tp', None), P(None)),
                         check_vma=False)
```

time: 1380 us -> 608 us (0.44)
  waiting for transfers between devices: 564 us -> 12.9 us
  matrix products: 515 us -> 0 us
  Pallas kernels: 0 us -> 475 us
  local copies, waits for them, and re-layouts: 168 us -> 15.1 us
  other arithmetic: 91.8 us -> 42.6 us
    psum x2 -> x1, waiting for transfers between devices: 564 us -> 0.02 us  [run(): lax.psum(jnp.where(me == 0, d0, d1) + swap(jnp.where(me == 0, d1, d0)), '...]
    dot_general x3 -> x0, matrix products: 515 us -> none  [the longest x1 189 us: local_step(): jnp.einsum('bsv,bsd->vd', grad_logits, normed, preferred_element_type=jnp...]
    pallas_call x0 -> x4, Pallas kernels: none -> 475 us  [the longest x1 134 us: run(): call(_own_kernel, 'grads_first', 2, base_own, sent, [log_spec] + own_ins,...]
    unnamed x21 -> x24, local copies, waits for them, and re-layouts: 168 us -> 0.07 us
    reduce_sum x4 -> x6, other arithmetic: 81.5 us -> 6.85 us  [the longest x1 3.93 us: local_step(): d_gain = (d_normed * x_hat).sum(0)]
    select_n x0 -> x3, other arithmetic: none -> 17.6 us  [the longest x1 13.5 us: pack(): return jnp.where(first, jnp.concatenate([a, zero], 0), moved)]
    psum x3 -> x0, blocking collectives: 14.5 us -> none  [the longest x1 8.21 us: local_step(): exp_sum = lax.psum(jnp.exp(logits - peak[..., None]).sum(-1), 'tp')]
    all_gather x0 -> x1, blocking collectives: none -> 14.1 us  [run(): stats = lax.all_gather(jnp.stack([m_dev, s_dev, tl.sum(0)]), ('tp', 'dp'))]
  transfers between devices with their start and end apart: 2 -> 7, of which waited for: 1 -> 2; matrix products, arithmetic and copies ran while one was open for 14% -> 2% of each run, Pallas kernels for 0% -> 37%
where the time goes in v1:
time: 608 us; the launch traced here: 599 us
  Pallas kernels  475 us (78%)
  other arithmetic  42.6 us (7%)
  between operations  17.5 us (3%)
  local copies, waits for them, and re-layouts  15.1 us (2%)
  blocking collectives  14.1 us (2%)
  loops' own time  13.6 us (2%)
  waiting for transfers between devices  12.9 us (2%)
  starting transfers between devices  8.51 us (1%)
    pallas_call x1, Pallas kernels, run(): call(_own_kernel, 'grads_first', 2, base_own, sent, [log_spec] + own_ins,...  134 us
    pallas_call x1, Pallas kernels, run(): call(_logits_kernel, 'logits', 1, base_own, half, [emb_spec, yft_spec, ve...  119 us
    pallas_call x1, Pallas kernels, run(): call(_own_kernel, 'grads_own', 2, base_own, half - sent, [later_spec] + o...  113 us
    pallas_call x1, Pallas kernels, run(): call(_peer_kernel, 'grads_peer', 2, base_peer, half - sent, [pl.BlockSpec...  109 us
    all_gather x1, blocking collectives, run(): stats = lax.all_gather(jnp.stack([m_dev, s_dev, tl.sum(0)]), ('tp', 'dp'))  14.1 us
    another operation x1, loops' own time, local_step(): lax.switch(which, [branch(n) for n in sizes], yf, tok_scale, local_ids, e...  13.6 us
    select_n x1, other arithmetic, pack(): return jnp.where(first, jnp.concatenate([a, zero], 0), moved)  13.5 us
  transfers between devices with their start and end apart: 7, of which 2 were waited for; matrix products, arithmetic and copies ran while one was open for 2% of the time, Pallas kernels for 37%

profile of v1, /device:TPU:0, one launch (start us, length us, event | category | flops | bytes accessed | tf_op | source)
XLA Modules:
  0.0 598.8 jit_solution(10754463038809075996)
XLA Ops:
  7.2 0.0 copy-start
  7.2 2.1 convert_reduce_fusion
  9.3 0.0 copy-start.8
  9.3 0.0 copy-start.14
  9.3 0.0 copy-start.16
  9.3 0.0 copy-start.12
  9.3 2.3 fusion.32
  11.6 0.0 copy-start.10
  11.6 2.5 fusion.30
  14.1 0.9 collective-permute-start.9
  15.0 0.0 copy-done.14
  15.0 0.0 collective-permute-start.8
  15.0 0.5 collective-permute-start.10
  15.5 0.6 broadcast_compare_fusion
  16.1 5.7 collective-permute-done.8
  21.8 0.6 fusion.46
  25.1 0.0 collective-permute-done.10
  25.1 0.1 fusion.45
  25.2 0.1 fusion.41
  25.3 0.0 collective-permute-done.9
  25.3 0.0 copy-done.8
  25.3 3.0 multiply_convert_fusion.2
  28.3 0.3 broadcast_in_dim.51
  28.6 13.5 %fusion.35 = bf16[2048,1024]{1,0:T(8,128)(2,1)} fusion(s32[]{:T(128)S(6)} %select_n.123, bf16[1024,1024]{1,0:T(8,128)(2,1)S(1)} %broadcast_in_dim.51, bf16[1024,1024]{1,0:T(8,128)(2,1)S(1)} %get-tuple-element.202, bf16[1024,1024]{1,0:T(8,128)(2,1)S(1)} %get-tuple-element.201, pred[2048]{0:T(1024)(128)(4,1)S(1)} %iota_compare_fusion), kind=kLoop, calls=%fused_computation.86 | loop fusion | flops 14680064 | bytes 10487812 | tf_op jit(solution)/shard_map/jit(_where)/select_n | solution.py:215
  42.1 529.6 %conditional.1 = (f32[62528,1024]{1,0:T(8,128)}, f32[1024,1024]{0,1:T(8,128)}, f32[]{:T(128)}) conditional(s32[]{:T(128)} %clamp.3, (bf16[2048,1024]{1,0:T(8,128)(2,1)}, s32[2048]{0:T(1024)S(1)}, s32[1]{0:T(128)}, bf16[62528,1024]{1,0:T(8,128)(2,1)}, f32[2048]{0:T(1024)S(1)}, /*index=5*/s32[1]{0:T(128)}, s32[]{:T(128)}, ...), branch_computations={%region_4.13_spmd, %region_13.0_spmd, %region_22.31_spmd, %region_... | conditional | flops 502515564544 | bytes 1674854400 | solution.py:296
  46.4 0.0 copy-start.6
  46.4 0.0 all-reduce.13.cloned.1.call-start
  46.4 0.5 copy-done.4
  47.0 0.0 copy-done.6
  47.0 4.4 fusion.51
  51.4 2.9 copy.32.yft_ref
  54.4 0.6 broadcast_in_dim.28.tgt_ref
  55.0 118.9 %logits.5 = (f32[31744,1536]{1,0:T(8,128)}, f32[8,1536]{1,0:T(8,128)}, f32[8,1536]{1,0:T(8,128)}, f32[8,1536]{1,0:T(8,128)}) custom-call(s32[1]{0:T(128)} %get-tuple-element.85.base_ref, bf16[62528,1024]{1,0:T(8,128)(2,1)} %get-tuple-element.84.emb_ref, bf16[1024,1536]{1,0:T(8,128)(2,1)} %copy.32.yft_ref, s32[8,1536]{1,0:T(8,128)} %broadcast_in_dim.28.tgt_ref), custom_call_target="tpu_custom_call" | custom-call | flops 99857989632 | bytes 455081984 | tf_op jit(solution)/shard_map/cond/branch_1_fun/logits/pallas_call | solution.py:255
  174.0 0.8 reduce_sum.218
  174.8 0.8 reduce_max.66
  175.6 0.9 multiply_reduce_fusion.1
  176.5 14.1 %all-gather.5 = f32[8,3,1536]{2,1,0:T(4,128)S(1)} all-gather(f32[1,3,1536]{2,1,0:T(4,128)S(1)} %maximum_bitcast_fusion.1), channel_id=3, replica_groups=mesh['tp'=4,'dp'=2] {'tp','dp'}, dimensions={0}, use_global_device_ids=true | all-gather | bytes 165888 | tf_op jit(solution)/shard_map/cond/branch_1_fun/all_gather | solution.py:261
  190.6 0.1 fusion.52
  190.8 0.0 copy-done.5
  190.8 0.6 fusion.13
  191.5 0.7 stack.80.vec_ref
  192.2 134.2 %grads_first.5 = (f32[62528,1024]{1,0:T(8,128)}, f32[1024,1536]{1,0:T(8,128)}, f32[17408,1024]{1,0:T(8,128)}) custom-call(s32[1]{0:T(128)} %get-tuple-element.85.base_ref, f32[31744,1536]{1,0:T(8,128)} %get-tuple-element.88.log_ref, bf16[62528,1024]{1,0:T(8,128)(2,1)} %get-tuple-element.84.emb_ref, bf16[1536,1024]{1,0:T(8,128)(2,1)} %get-tuple-element.181.yf_ref, ...), custom_call_target="tpu_custom_call" | custom-call | flops 109521666048 | bytes 249561088 | tf_op jit(solution)/shard_map/cond/branch_1_fun/grads_first/pallas_call | solution.py:271
  326.3 0.0 collective-permute-start.2
  326.4 112.9 %grads_own.5 = (f32[62528,1024]{1,0:T(8,128)}, f32[1024,1536]{1,0:T(8,128)}) custom-call(s32[1]{0:T(128)S(6)} %add.137.base_ref, f32[31744,1536]{1,0:T(8,128)} %get-tuple-element.88.log_ref, bf16[62528,1024]{1,0:T(8,128)(2,1)} %get-tuple-element.84.emb_ref, bf16[1536,1024]{1,0:T(8,128)(2,1)} %get-tuple-element.181.yf_ref, ...), custom_call_target="tpu_custom_call", output_to_operand_aliasing={{0}: (6, {})} | custom-call | flops 90194313216 | bytes 205520896 | tf_op jit(solution)/shard_map/cond/branch_1_fun/grads_own/pallas_call | solution.py:276
  439.3 0.0 slice-start.3
  439.3 4.1 slice_select_fusion.1
  443.4 0.0 collective-permute-start.3
  443.4 7.1 %collective-permute-done.3 = f32[1024,1024]{0,1:T(8,128)S(1)} collective-permute-done((f32[1024,1024]{0,1:T(8,128)S(1)}, f32[1024,1024]{0,1:T(8,128)S(1)}, u32[]{:S(2)}, u32[]{:S(2)}) %collective-permute-start.3) | collective-permute-done | bytes 4194336 | tf_op jit(solution)/shard_map/cond/branch_1_fun/ppermute | solution.py:282
  450.6 3.3 select_add_fusion.1
  453.9 0.0 all-reduce.13.cloned.1.call-update
  453.9 0.0 collective-permute-done.2.got_ref
  453.9 108.6 %grads_peer.5 = f32[62528,1024]{1,0:T(8,128)} custom-call(s32[1]{0:T(128)} %get-tuple-element.83.base_ref, bf16[62528,1024]{1,0:T(8,128)(2,1)} %get-tuple-element.84.emb_ref, f32[17408,1024]{1,0:T(8,128)} %collective-permute-done.2.got_ref, bf16[1024,1536]{1,0:T(8,128)(2,1)} %copy.32.yft_ref, ...), custom_call_target="tpu_custom_call", output_to_operand_aliasing={{}: (7, {})} | custom-call | flops 90194313216 | bytes 205520896 | tf_op jit(solution)/shard_map/cond/branch_1_fun/grads_peer/pallas_call | solution.py:283
  562.5 0.0 all-reduce.13.cloned.1.call-done
  571.6 0.0 copy-start.1
  571.7 0.0 copy-start.11
  571.7 0.0 copy-start.13
  571.7 0.0 copy-start.15
  571.7 5.5 copy.40
  577.2 0.0 copy-done.9
  577.2 3.9 multiply_reduce_fusion.4
  581.2 7.1 %collective-permute-start.11 = (f32[1024]{0:T(1024)S(1)}, f32[1024]{0:T(1024)S(1)}, u32[]{:S(2)}, u32[]{:S(2)}) collective-permute-start(f32[1024]{0:T(1024)S(1)} %get-tuple-element.158), channel_id=1, source_target_pairs={{0,1},{1,0},{2,3},{3,2},{4,5},{5,4},{6,7},{7,6}} | collective-permute-start | bytes 12296 | tf_op jit(solution)/shard_map/ppermute | solution.py:300
  588.3 2.6 fusion.37
  590.8 0.0 collective-permute-done.11
  590.8 0.6 add.174
  (35 shorter events, 0.2 us)
Async XLA Ops:
  7.2 4.5 copy-start
  9.3 16.0 %copy-start.8 = (f32[1024]{0:T(1024)}, f32[1024]{0:T(1024)S(1)}, u32[]{:S(2)}) copy-start(f32[1024]{0:T(1024)S(1)} %broadcast_multiply_fusion.2) | copy-start | bytes 12292
  9.3 5.7 copy-start.14
  9.3 5.7 copy-start.16
  9.3 16.0 %copy-start.12 = (f32[1024]{0:T(1024)S(1)}, f32[1024]{0:T(1024)}, u32[]{:S(2)}) copy-start(f32[1024]{0:T(1024)} %param.10) | copy-start | bytes 12292
  11.6 16.7 %copy-start.10 = (f32[1024]{0:T(1024)}, f32[1024]{0:T(1024)S(1)}, u32[]{:S(2)}) copy-start(f32[1024]{0:T(1024)S(1)} %add_rsqrt_fusion) | copy-start | bytes 12292
  14.1 11.1 %collective-permute-start.9 = (f32[1024,1024]{1,0:T(8,128)}, f32[1024,1024]{1,0:T(8,128)}, u32[]{:S(2)}, u32[]{:S(2)}) collective-permute-start(f32[1024,1024]{1,0:T(8,128)} %fusion.30), channel_id=1, source_target_pairs={{0,1},{1,0},{2,3},{3,2},{4,5},{5,4},{6,7},{7,6}} | collective-permute-start | bytes 12582920 | tf_op jit(solution)/shard_map/ppermute | solution.py:202
  15.0 6.8 %collective-permute-start.8 = (f32[1024]{0:T(1024)S(1)}, f32[1024]{0:T(1024)S(1)}, u32[]{:S(2)}, u32[]{:S(2)}) collective-permute-start(f32[1024]{0:T(1024)S(1)} %bitcast.139), channel_id=1, source_target_pairs={{0,1},{1,0},{2,3},{3,2},{4,5},{5,4},{6,7},{7,6}} | collective-permute-start | bytes 12296 | tf_op jit(solution)/shard_map/ppermute | solution.py:204
  15.0 10.1 %collective-permute-start.10 = (s32[1024]{0:T(1024)S(1)}, s32[1024]{0:T(1024)S(1)}, u32[]{:S(2)}, u32[]{:S(2)}) collective-permute-start(s32[1024]{0:T(1024)S(1)} %bitcast.142), channel_id=1, source_target_pairs={{0,1},{1,0},{2,3},{3,2},{4,5},{5,4},{6,7},{7,6}} | collective-permute-start | bytes 12296 | tf_op jit(solution)/shard_map/ppermute | solution.py:203
  46.4 0.6 copy-start.4
  46.4 0.6 copy-start.6
  46.4 516.2 %all-reduce.13.cloned.1.call-start = ((), (), s32[]{:S(2)}) async-start(), calls=%async_computation.1 | async-start | bytes 8388608 | tf_op jit(solution)/shard_map/cond/branch_1_fun/psum | solution.py:282
  51.4 3.0 copy-start.7
  55.0 135.8 %copy-start.5 = (f32[2048]{0:T(1024)S(1)}, f32[2048]{0:T(1024)}, u32[]{:S(2)}) copy-start(f32[2048]{0:T(1024)} %copy-done.4) | copy-start | bytes 24580 | tf_op jit(solution)/shard_map/cond
  326.3 127.6 %collective-permute-start.2 = (f32[17408,1024]{1,0:T(8,128)}, f32[17408,1024]{1,0:T(8,128)}, u32[]{:S(2)}, u32[]{:S(2)}) collective-permute-start(f32[17408,1024]{1,0:T(8,128)} %get-tuple-element.93), channel_id=1, source_target_pairs={{0,1},{1,0},{2,3},{3,2},{4,5},{5,4},{6,7},{7,6}} | collective-permute-start | bytes 213909504 | tf_op jit(solution)/shard_map/cond/branch_1_fun/ppermute | solution.py:275
  439.3 11.3 %slice-start.2 = ((s8[6291456]{0:T(1024)(128)(4,1)}), s8[4194304]{0:T(1024)(128)(4,1)S(1)}, s32[]{:S(2)}) async-start(s8[6291456]{0:T(1024)(128)(4,1)} %bitcast.114), calls=%async_computation.6 | async-start | bytes 8388608 | tf_op jit(solution)/shard_map/cond
  439.3 11.3 %slice-start.3 = ((s8[6291456]{0:T(1024)(128)(4,1)}), s8[2097152]{0:T(1024)(128)(4,1)S(1)}, s32[]{:S(2)}) async-start(s8[6291456]{0:T(1024)(128)(4,1)} %bitcast.114), calls=%async_computation.7 | async-start | bytes 4194304 | tf_op jit(solution)/shard_map/cond
  443.4 7.2 %collective-permute-start.3 = (f32[1024,1024]{0,1:T(8,128)S(1)}, f32[1024,1024]{0,1:T(8,128)S(1)}, u32[]{:S(2)}, u32[]{:S(2)}) collective-permute-start(f32[1024,1024]{0,1:T(8,128)S(1)} %slice_select_fusion.1), channel_id=1, source_target_pairs={{0,1},{1,0},{2,3},{3,2},{4,5},{5,4},{6,7},{7,6}} | collective-permute-start | bytes 12582920 | tf_op jit(solution)/shard_map/cond/branch_1_fun/ppermute | solution.py:282
  571.6 5.6 copy-start.1
  571.7 5.5 copy-start.9
  571.7 5.5 copy-start.11
  571.7 5.5 copy-start.13
  571.7 5.5 copy-start.15
  577.2 11.0 %copy-start.2 = (f32[1024,1024]{1,0:T(8,128)S(1)}, f32[1024,1024]{1,0:T(8,128)}, u32[]{:S(2)}) copy-start(f32[1024,1024]{1,0:T(8,128)} %copy.40) | copy-start | bytes 12582916
  581.2 9.7 %collective-permute-start.11 = (f32[1024]{0:T(1024)S(1)}, f32[1024]{0:T(1024)S(1)}, u32[]{:S(2)}, u32[]{:S(2)}) collective-permute-start(f32[1024]{0:T(1024)S(1)} %get-tuple-element.158), channel_id=1, source_target_pairs={{0,1},{1,0},{2,3},{3,2},{4,5},{5,4},{6,7},{7,6}} | collective-permute-start | bytes 12296 | tf_op jit(solution)/shard_map/ppermute | solution.py:300
Sparse Core Ops, SparseCore 0:
  454.0 91.9 all-reduce.12
